TPU v7x, 32 devices: a whole 2x2x4 slice. The times are simulated.
32 devices in a mesh: row: 4 (over x, core), col: 8 (over z, y).
Axes of the slice: x: 2, y: 2, z: 4, core: 2. Of those that a mesh axis runs over, the one named last changes fastest.
Arguments:
- right_sides: bfloat16 [1024, 64, 128], P(('row', 'col')), may hold values from -7 to 7
- weights_fine: bfloat16 [1024, 3, 128, 128], P(('row', 'col')), may hold values from 0 to 2
- columns_fine: int32 [1024, 3], P(('row', 'col')), may hold values from 0 to 1023, as said below
- degree_fine: float32 [1024, 128], P(('row', 'col')), may hold values from 0.05 to 0.5
- owners_fine: int32 [1024, 128], P(('row', 'col')), may hold values from 0 to 31, as said below
- slots_fine: int32 [1024, 128], P(('row', 'col')), may hold values from 0 to 1023
- weights_second: bfloat16 [256, 3, 128, 128], P(('row', 'col')), may hold values from 0 to 8
- columns_second: int32 [256, 3], P(('row', 'col')), may hold values from 0 to 255, as said below
- degree_second: float32 [256, 128], P(('row', 'col')), may hold values from 0.2 to 2
- owners_second: int32 [256, 128], P(('row', 'col')), may hold values from 0 to 31, as said below
- slots_second: int32 [256, 128], P(('row', 'col')), may hold values from 0 to 255
- weights_third: bfloat16 [64, 3, 128, 128], P(('row', 'col')), may hold values from 0 to 32
- columns_third: int32 [64, 3], P(('row', 'col')), may hold values from 0 to 63, as said below
- degree_third: float32 [64, 128], P(('row', 'col')), may hold values from 0.8 to 8
- owners_third: int32 [64, 128], P(('row', 'col')), may hold values from 0 to 31, as said below
- slots_third: int32 [64, 128], P(('row', 'col')), may hold values from 0 to 127
- coarse_inverse: bfloat16 [4096, 1024], P(('row', 'col')), may hold values from -1 to 1, as said below
Outputs:
- solution: float32 [1024, 64, 128], P(('row', 'col'))
Inputs may be any that keep to these rules, and one draw needn't show every extreme that they name: `columns_fine`: every entry lies within 2 blocks of its own row block's index, on the same level. `columns_second`: every entry lies within 2 blocks of its own row block's index, on the same level. `columns_third`: every entry lies within 2 blocks of its own row block's index, on the same level. `owners_fine`: each entry is the device holding the vertex or the one just before or after it in device order. `owners_second`: each entry is the device holding the vertex or the one just before or after it in device order. `owners_third`: each entry is the device holding the vertex or the one just before or after it in device order. `coarse_inverse`: each row group's block is symmetric.
All inputs are finite; a program needn't handle non-finite values.
Results may differ from a plain program's by a relative error of at most 0.0003.
Values may be sent and summed in bfloat16 or wider, within the bound.
A program may use at most 64 MiB of HBM per device.

v0:
```python
import functools

import jax
import jax.numpy as jnp
from jax import lax
from jax.experimental import pallas as pl
from jax.experimental.pallas import tpu as pltpu
from jax.sharding import PartitionSpec as P

F32 = jnp.float32
BF16 = jnp.bfloat16
MESH = pl.DeviceIdType.MESH
DAMPING = 0.8
SPLIT_OWN = False


def loop(low, high, body, unroll=4):
    count = high - low
    if count <= 0:
        return
    while count % unroll:
        unroll -= 1

    if count == unroll:
        for inner in range(count):
            body(low + inner)
        return

    def step(outer, carry):
        for inner in range(unroll):
            body(low + outer * unroll + inner)
        return carry

    lax.fori_loop(0, count // unroll, step, 0)


def grouped(low, high, first, then, unroll=7):
    count = high - low
    if count <= 0:
        return
    while count % unroll:
        unroll -= 1

    def group(start):
        made = [first(start + inner) for inner in range(unroll)]
        for inner in range(unroll):
            then(start + inner, made[inner])

    if count == unroll:
        group(low)
        return

    def step(outer, carry):
        group(low + outer * unroll)
        return carry

    lax.fori_loop(0, count // unroll, step, 0)


class Level:
    def __init__(self, blocks, coarse, rhs_count, bs, k, ref, hbm, columns, ops):
        self.n, self.t, self.r, self.bs, self.k = blocks, coarse, rhs_count, bs, k
        self.ref, self.hbm, self.columns, self.ops = ref, hbm, columns, ops
        self.single = blocks < 4
        self.base = ops.me * blocks
        self.scale = 1.0 / (k * bs)

    def edges(self):
        n = self.n
        if self.single:
            return list(range(n))
        return [0, 1, n - 2, n - 1]

    def inner(self):
        return (0, 0) if self.single else (2, self.n - 2)

    def weight_sums(self, b):
        w = self.ref["w"][b]
        return jnp.dot(jnp.ones((8, w.shape[0]), BF16), w, preferred_element_type=F32)

    def put_diagonal(self, b, total):
        degree = self.ref["deg"][pl.ds(b, 1), :]
        g = degree + total * self.scale
        self.ref["g"][b] = g
        self.ref["gi"][b] = DAMPING / g

    def row(self, name, b):
        value = self.ref[name][b, 0:1, :]
        return jnp.broadcast_to(value, (self.r, self.bs))

    def f(self, b):
        return self.ref["f"][b].astype(F32)

    def product(self, i, b, where):
        if where == "inner":
            buf, offset = self.ref[f"vb{i}"], self.base
        elif where == "low":
            buf, offset = self.ref[f"lo{i}"], self.base - 2
        else:
            buf, offset = self.ref[f"hi{i}"], self.base + self.n - 4
        top = buf.shape[0] - 1
        picked = [
            buf[jnp.clip(self.columns[b, k] - offset, 0, top)] for k in range(self.k)
        ]
        left = jnp.concatenate(picked, axis=1)
        return jnp.dot(left, self.ref["w"][b], preferred_element_type=F32) * self.scale

    def halo_copies(self, i):
        n, ops, vb = self.n, self.ops, self.ref[f"vb{i}"]
        if self.single:
            low_dst, high_dst = self.ref[f"lo{i}"].at[0:2], self.ref[f"lo{i}"].at[4:6]
        else:
            low_dst, high_dst = self.ref[f"lo{i}"].at[0:2], self.ref[f"hi{i}"].at[4:6]
        return ops.pair(vb.at[n - 2 : n], low_dst, vb.at[0:2], high_dst, self.ref["sem"] + i)

    def fill_edges(self, i):
        n = self.n
        if self.single:
            self.ref[f"lo{i}"][2:4] = self.ref[f"vb{i}"][0:2]
        else:
            self.ref[f"lo{i}"][2:6] = self.ref[f"vb{i}"][0:4]
            self.ref[f"hi{i}"][0:4] = self.ref[f"vb{i}"][n - 4 : n]

    def run_edges(self, i, body):
        made = [self.product(i, b, "low" if b < 2 else "high") for b in self.edges()]
        for b, product in zip(self.edges(), made):
            body(b, product)

    def apply(self, i, body):
        grouped(*self.inner(), lambda b: self.product(i, b, "inner"), body)
        self.fill_edges(i)
        self.ops.wait(self.halo_copies(i))
        self.run_edges(i, body)

    def start_block(self, b):
        self.ref["vb0"][b] = (self.row("gi", b) * self.f(b)).astype(BF16)

    def first_sweep(self, b, product):
        f, gi = self.f(b), self.row("gi", b)
        x0 = gi * f
        x = (1.0 - DAMPING) * x0 + gi * (f + product)
        self.ref["x"][b] = x
        self.ref["vb1"][b] = x.astype(BF16)

    def residual(self, b, product):
        res = self.f(b) - self.row("g", b) * self.ref["x"][b] + product
        rel = self.owner(b)
        columns = pl.ds(pl.multiple_of(b * self.bs, self.bs), self.bs)
        rows = self.r
        high = res.astype(BF16)
        zero = jnp.zeros_like(res)
        out = self.ref["res"]
        out[0:rows, columns] = jnp.where(rel < 0, res, zero).astype(BF16)
        out[rows : 2 * rows, columns] = jnp.where(rel > 0, res, zero).astype(BF16)
        own = jnp.where(rel == 0, res, zero)
        high = own.astype(BF16)
        out[2 * rows : 3 * rows, columns] = high
        if SPLIT_OWN:
            out[3 * rows : 4 * rows, columns] = (own - high.astype(F32)).astype(BF16)

    def owner(self, b):
        value = self.ref["own"][pl.ds(b, 1), :] - self.ops.me
        return jnp.broadcast_to(value, (self.r, self.bs))

    def make_onehot(self, b):
        columns = pl.ds(pl.multiple_of(b * self.bs, self.bs), self.bs)
        slots = jnp.broadcast_to(self.ref["slot"][pl.ds(b, 1), :], (self.t, self.bs))
        index = lax.broadcasted_iota(jnp.int32, (self.t, self.bs), 0)
        self.ref["oh"][:, columns] = jnp.where(index == slots, 1.0, 0.0).astype(BF16)

    def restricted(self, rows, put):
        tile = min(self.t, 256)

        def body(j):
            at = pl.ds(pl.multiple_of(j * tile, tile), tile)
            put(
                at,
                lax.dot_general(
                    self.ref["res"][rows, :],
                    self.ref["oh"][at, :],
                    (((1,), (1,)), ((), ())),
                    preferred_element_type=F32,
                ),
            )

        loop(0, self.t // tile, body, 1)

    def restrict_copies(self):
        out, got = self.ref["rout"], self.ref["rin"]
        return self.ops.pair(out.at[1], got.at[0], out.at[0], got.at[1], self.ref["sem"] + 4)

    def restrict(self, into):
        r = self.r

        def put_out(at, value):
            self.ref["rout"][0, :, at] = value[0:r].astype(BF16)
            self.ref["rout"][1, :, at] = value[r : 2 * r].astype(BF16)

        self.restricted(slice(0, 2 * r), put_out)
        copies = self.restrict_copies()
        self.ops.start(copies)

        def put_own(at, value):
            if SPLIT_OWN:
                value = value[0:r] + value[r : 2 * r]
            self.ref["rown"][:, at] = value

        self.restricted(slice(2 * r, (4 if SPLIT_OWN else 3) * r), put_own)
        self.ops.wait(copies)
        for block in range(self.t // self.bs):
            at = slice(block * self.bs, (block + 1) * self.bs)
            into(
                block,
                self.ref["rown"][:, at]
                + self.ref["rin"][0, :, at].astype(F32)
                + self.ref["rin"][1, :, at].astype(F32),
            )

    def down(self, into, while_first=None, while_second=None):
        self.ops.start(self.halo_copies(0))
        loop(*self.inner(), self.start_block)
        if while_first is not None:
            while_first()
        self.apply(0, self.first_sweep)
        self.ops.start(self.halo_copies(1))
        if while_second is not None:
            while_second()
        self.apply(1, self.residual)
        self.restrict(into)

    def prolong_copies(self):
        out, got = self.ref["uout"], self.ref["uin"]
        return self.ops.pair(out, got.at[0], out, got.at[1], self.ref["sem"] + 5)

    def pair_columns(self, pair):
        return pl.ds(pl.multiple_of(pair * 2 * self.bs, 2 * self.bs), 2 * self.bs)

    def own_part(self, pair):
        return jnp.dot(
            self.ref["uout"][...], self.ref["oh"][:, self.pair_columns(pair)],
            preferred_element_type=F32,
        )

    def add_own(self, pair, value):
        for half in range(2):
            b = 2 * pair + half
            part = value[:, half * self.bs : (half + 1) * self.bs]
            self.ref["x"][b] = self.ref["x"][b] + jnp.where(self.owner(b) == 0, part, 0.0)

    def others_part(self, pair):
        left = jnp.concatenate([self.ref["uin"][0], self.ref["uin"][1]], axis=0)
        return jnp.dot(
            left, self.ref["oh"][:, self.pair_columns(pair)], preferred_element_type=F32
        )

    def add_others(self, pair, value):
        for half in range(2):
            b = 2 * pair + half
            at = slice(half * self.bs, (half + 1) * self.bs)
            rel = self.owner(b)
            x = self.ref["x"][b]
            x = x + jnp.where(rel < 0, value[0 : self.r, at], 0.0)
            x = x + jnp.where(rel > 0, value[self.r : 2 * self.r, at], 0.0)
            self.ref["x"][b] = x
            self.ref["vb2"][b] = x.astype(BF16)

    def sweep(self, i, last, out=None):
        def body(b, product):
            gi = self.row("gi", b)
            x = (1.0 - DAMPING) * self.ref["x"][b] + gi * (self.f(b) + product)
            self.ref["x"][b] = x
            if not last:
                self.ref[f"vb{i + 1}"][b] = x.astype(BF16)
            elif out is not None:
                out(b, x)

        return body

    def up(self, out=None):
        copies = self.prolong_copies()
        self.ops.start(copies)
        pairs = self.n // 2
        grouped(0, pairs, self.own_part, self.add_own, 2)
        self.ops.wait(copies)
        ends = [0] if self.single else [0, pairs - 1]
        made = [self.others_part(pair) for pair in ends]
        for pair, value in zip(ends, made):
            self.add_others(pair, value)
        self.ops.start(self.halo_copies(2))
        if not self.single:
            grouped(1, pairs - 1, self.others_part, self.add_others, 2)
        self.apply(2, self.sweep(2, False))
        self.ops.start(self.halo_copies(3))
        self.apply(3, self.sweep(3, True, out))

    def drain(self):
        for i in range(4):
            self.ops.drain(self.halo_copies(i))
        self.ops.drain(self.restrict_copies())
        self.ops.drain(self.prolong_copies())

    def clear_ends(self):
        for name, first, last in (("rin", 0, 1), ("uin", 0, 1)):
            ref = self.ref[name]

            @pl.when(self.ops.me == 0)
            def _():
                ref[first] = jnp.zeros(ref.shape[1:], ref.dtype)

            @pl.when(self.ops.me == self.ops.total - 1)
            def _():
                ref[last] = jnp.zeros(ref.shape[1:], ref.dtype)


class Ops:
    def __init__(self, send, recv):
        self.send, self.recv = send, recv
        self.rows, self.cols = lax.axis_size("row"), lax.axis_size("col")
        self.total = self.rows * self.cols
        self.row, self.col = lax.axis_index("row"), lax.axis_index("col")
        self.me = self.row * self.cols + self.col
        right = jnp.minimum(self.me + 1, self.total - 1)
        left = jnp.maximum(self.me - 1, 0)
        self.right = (right // self.cols, right % self.cols)
        self.left = (left // self.cols, left % self.cols)
        self.has_right = self.me < self.total - 1
        self.has_left = self.me > 0

    def pair(self, to_right, at_right, to_left, at_left, slot):
        first = pltpu.make_async_remote_copy(
            to_right, at_right, self.send.at[slot, 0], self.recv.at[slot, 0],
            device_id=self.right, device_id_type=MESH,
        )
        second = pltpu.make_async_remote_copy(
            to_left, at_left, self.send.at[slot, 1], self.recv.at[slot, 1],
            device_id=self.left, device_id_type=MESH,
        )
        return first, second

    def start(self, copies):
        pl.when(self.has_right)(lambda: copies[0].start())
        pl.when(self.has_left)(lambda: copies[1].start())

    def wait(self, copies):
        pl.when(self.has_left)(lambda: copies[0].wait_recv())
        pl.when(self.has_right)(lambda: copies[1].wait_recv())

    def drain(self, copies):
        pl.when(self.has_right)(lambda: copies[0].wait_send())
        pl.when(self.has_left)(lambda: copies[1].wait_send())


LEVEL_HBM = ("w", "deg", "own", "slot")
LEVEL_SCRATCH = (
    "w", "deg", "own", "slot", "g", "gi", "x", "vb0", "vb1", "vb2", "vb3",
    "lo0", "lo1", "lo2", "lo3", "hi0", "hi1", "hi2", "hi3", "res", "oh",
    "rout", "rin", "rown", "uout", "uin",
)


def kernel(sizes, rhs_count, bs, k, coarse_all, *refs):
    refs = list(refs)
    take = lambda count: [refs.pop(0) for _ in range(count)]
    rhs_hbm, inverse_hbm = take(2)
    columns, hbm = [], []
    for _ in sizes:
        columns.append(refs.pop(0))
        hbm.append(dict(zip(LEVEL_HBM, take(4))))
    (out_hbm,) = take(1)
    scratch = [dict(zip(LEVEL_SCRATCH, take(len(LEVEL_SCRATCH)))) for _ in sizes]
    rhs, f_second, f_third, inverse, gathered, out = take(6)
    send, recv, gather_send, gather_recv, local, out_sem = take(6)

    ops = Ops(send, recv)
    levels = []
    for position, (n, t) in enumerate(sizes):
        ref = scratch[position]
        ref["sem"] = position * 6
        ref["f"] = (rhs, f_second, f_third)[position]
        levels.append(Level(n, t, rhs_count, bs, k, ref, hbm[position], columns[position], ops))
    fine, second, third = levels

    loads = []

    def load(src, dst):
        copy = pltpu.make_async_copy(src, dst, local.at[len(loads)])
        loads.append(copy)
        copy.start()
        return copy

    n = fine.n
    early = []
    for at in (slice(0, 2), slice(n - 2, n)):
        early.append(load(hbm[0]["w"].at[at], scratch[0]["w"].at[at]))
    early.append(load(hbm[0]["deg"], scratch[0]["deg"]))
    early.append(load(rhs_hbm, rhs))
    middle = load(hbm[0]["w"].at[2 : n - 2], scratch[0]["w"].at[2 : n - 2])
    later = [
        load(hbm[0][name], scratch[0][name]) for name in ("own", "slot")
    ]
    for position in (1, 2):
        later += [load(hbm[position][name], scratch[position][name]) for name in LEVEL_HBM]
    later.append(load(inverse_hbm, inverse))

    barrier = pltpu.get_barrier_semaphore()
    next_row = jnp.logical_and(ops.has_right, ops.col == ops.cols - 1)
    previous_row = jnp.logical_and(ops.has_left, ops.col == 0)
    pl.when(next_row)(
        lambda: pl.semaphore_signal(barrier, inc=1, device_id=ops.right, device_id_type=MESH)
    )
    pl.when(previous_row)(
        lambda: pl.semaphore_signal(barrier, inc=1, device_id=ops.left, device_id_type=MESH)
    )
    for step in range(1, ops.cols):
        peer = lax.rem(ops.col + step, ops.cols)
        pl.semaphore_signal(barrier, inc=1, device_id=(ops.row, peer), device_id_type=MESH)
    for level in levels:
        level.clear_ends()
    for copy in early:
        copy.wait()
    def diagonal_and_start(b, total):
        fine.put_diagonal(b, total)
        fine.start_block(b)

    made = [fine.weight_sums(b) for b in fine.edges()]
    for b, total in zip(fine.edges(), made):
        diagonal_and_start(b, total)
    pl.semaphore_wait(
        barrier, ops.cols - 1 + next_row.astype(jnp.int32) + previous_row.astype(jnp.int32)
    )

    fine.ops.start(fine.halo_copies(0))
    middle.wait()

    grouped(*fine.inner(), fine.weight_sums, diagonal_and_start)
    for copy in later:
        copy.wait()
    loop(0, fine.n // 2, fine.make_onehot, 1)
    fine.apply(0, fine.first_sweep)
    fine.ops.start(fine.halo_copies(1))
    loop(fine.n // 2, fine.n, fine.make_onehot, 1)
    for level in (second, third):
        loop(0, level.n, level.make_onehot, 1)
        grouped(0, level.n, level.weight_sums, level.put_diagonal, 8)
    fine.apply(1, fine.residual)

    def into_level(level):
        def into(block, value):
            level.ref["f"][block] = value

        return into

    fine.restrict(into_level(second))
    for level, following in ((second, third), (third, None)):
        for b in level.edges():
            level.start_block(b)
        if following is not None:
            level.down(into_level(following))
        else:

            def into_coarse(block, value):
                gathered[ops.col] = value.astype(BF16)

            level.down(into_coarse)

    sends = []
    for step in range(1, ops.cols):
        peer = lax.rem(ops.col + step, ops.cols)
        copy = pltpu.make_async_remote_copy(
            gathered.at[ops.col], gathered.at[ops.col],
            gather_send.at[step - 1], gather_recv.at[step - 1],
            device_id=(ops.row, peer), device_id_type=MESH,
        )
        copy.start()
        sends.append(copy)
    for step in range(1, ops.cols):
        source = lax.rem(ops.col + ops.cols - step, ops.cols)
        pltpu.make_async_remote_copy(
            gathered.at[source], gathered.at[source],
            gather_send.at[step - 1], gather_recv.at[step - 1],
            device_id=(ops.row, source), device_id_type=MESH,
        ).wait_recv()
    everything = jnp.concatenate([gathered[p] for p in range(ops.cols)], axis=1)
    solved = lax.dot_general(
        everything, inverse[...], (((1,), (1,)), ((), ())), preferred_element_type=F32
    )
    third.ref["uout"][...] = solved.astype(BF16)

    def into_coarse_vector(level):
        def put(b, x):
            level.ref["uout"][:, b * bs : (b + 1) * bs] = x.astype(BF16)

        return put

    third.up(into_coarse_vector(second))
    second.up(into_coarse_vector(fine))

    def put_out(b, x):
        out[b] = x

    fine.up(put_out)
    result = pltpu.make_async_copy(out, out_hbm, out_sem.at[0])
    result.start()
    for level in levels:
        level.drain()
    for copy in sends:
        copy.wait_send()
    result.wait()


def on_device(
    right_sides,
    weights_fine, columns_fine, degree_fine, owners_fine, slots_fine,
    weights_second, columns_second, degree_second, owners_second, slots_second,
    weights_third, columns_third, degree_third, owners_third, slots_third,
    coarse_inverse,
):
    n0, r, bs = right_sides.shape
    n1, n2 = weights_second.shape[0], weights_third.shape[0]
    k = weights_fine.shape[1]
    c3, m3 = coarse_inverse.shape
    cols = lax.axis_size("col")
    sizes = ((n0, n1 * bs), (n1, n2 * bs), (n2, c3))
    merged = lambda w: w.reshape(w.shape[0], k * bs, bs)
    args = [right_sides, coarse_inverse]
    specs = [pl.BlockSpec(memory_space=pl.ANY)] * 2
    for w, c, d, o, s in (
        (weights_fine, columns_fine, degree_fine, owners_fine, slots_fine),
        (weights_second, columns_second, degree_second, owners_second, slots_second),
        (weights_third, columns_third, degree_third, owners_third, slots_third),
    ):
        args += [c, merged(w), d, o, s]
        specs += [pl.BlockSpec(memory_space=pltpu.SMEM)]
        specs += [pl.BlockSpec(memory_space=pl.ANY)] * 4
    scratch = []
    for n, t in sizes:
        scratch += [
            pltpu.VMEM((n, k * bs, bs), BF16),
            pltpu.VMEM((n, bs), F32),
            pltpu.VMEM((n, bs), jnp.int32),
            pltpu.VMEM((n, bs), jnp.int32),
            pltpu.VMEM((n, 8, bs), F32),
            pltpu.VMEM((n, 8, bs), F32),
            pltpu.VMEM((n, r, bs), F32),
            *[pltpu.VMEM((n, r, bs), BF16)] * 4,
            *[pltpu.VMEM((6, r, bs), BF16)] * 8,
            pltpu.VMEM(((4 if SPLIT_OWN else 3) * r, n * bs), BF16),
            pltpu.VMEM((t, n * bs), BF16),
            pltpu.VMEM((2, r, t), BF16),
            pltpu.VMEM((2, r, t), BF16),
            pltpu.VMEM((r, t), F32),
            pltpu.VMEM((r, t), BF16),
            pltpu.VMEM((2, r, t), BF16),
        ]
    scratch += [
        pltpu.VMEM((n0, r, bs), BF16),
        pltpu.VMEM((n1, r, bs), F32),
        pltpu.VMEM((n2, r, bs), F32),
        pltpu.VMEM((c3, m3), BF16),
        pltpu.VMEM((cols, r, c3), BF16),
        pltpu.VMEM((n0, r, bs), F32),
        pltpu.SemaphoreType.DMA((18, 2)),
        pltpu.SemaphoreType.DMA((18, 2)),
        pltpu.SemaphoreType.DMA((cols,)),
        pltpu.SemaphoreType.DMA((cols,)),
        pltpu.SemaphoreType.DMA((24,)),
        pltpu.SemaphoreType.DMA((1,)),
    ]
    return pl.pallas_call(
        functools.partial(kernel, sizes, r, bs, k, m3),
        out_shape=jax.ShapeDtypeStruct((n0, r, bs), F32),
        in_specs=specs,
        out_specs=pl.BlockSpec(memory_space=pl.ANY),
        scratch_shapes=scratch,
        compiler_params=pltpu.CompilerParams(
            collective_id=0, has_side_effects=True, vmem_limit_bytes=48 * 1024 * 1024
        ),
        name="vcycle",
    )(*args)


def solution(mesh):
    whole = ("row", "col")
    vector, matrix, table = P(whole, None, None), P(whole, None, None, None), P(whole, None)
    level = (matrix, table, table, table, table)
    return jax.shard_map(
        on_device,
        mesh=mesh,
        in_specs=(vector, *level, *level, *level, table),
        out_specs=vector,
        check_vma=False,
    )
```

profile of v0, /device:TPU:3, one launch (start us, length us, event | category | flops | bytes accessed | tf_op | source)
XLA Modules:
  0.0 112.2 jit_solution(3213295669926479480)
XLA Ops:
  0.0 0.8 copy.19.refs_7_
  0.8 0.8 copy.18.refs_2_
  1.5 0.0 copy-start
  1.5 1.9 %copy-done = bf16[32,3,128,128]{3,2,1,0:T(8,128)(2,1)S(1)} copy-done((bf16[32,3,128,128]{3,2,1,0:T(8,128)(2,1)S(1)}, bf16[32,3,128,128]{3,2,1,0:T(8,128)(2,1)}, u32[]{:S(2)}) %copy-start) | copy-done | bytes 3145752
  3.4 0.0 copy-start.1
  3.4 1.1 %copy-done.1 = bf16[8,3,128,128]{3,2,1,0:T(8,128)(2,1)S(1)} copy-done((bf16[8,3,128,128]{3,2,1,0:T(8,128)(2,1)S(1)}, bf16[8,3,128,128]{3,2,1,0:T(8,128)(2,1)}, u32[]{:S(2)}) %copy-start.1) | copy-done | bytes 786456
  4.5 0.0 copy-start.2
  4.5 1.0 copy-done.2
  5.6 0.0 copy-start.3
  5.6 0.9 copy-done.3
  6.5 0.0 copy-start.4
  6.5 0.9 copy-done.4
  7.5 0.0 copy-start.5
  7.5 0.7 copy-done.5
  8.2 0.0 copy-start.6
  8.2 0.7 copy-done.6
  8.9 0.0 copy-start.7
  8.9 0.7 copy-done.7
  9.6 0.0 copy-start.8
  9.6 0.7 copy-done.8
  10.3 0.0 copy-start.9
  10.3 0.7 copy-done.9
  11.0 0.0 copy-start.10
  11.0 0.7 copy-done.10
  11.7 0.0 copy-start.11
  11.7 0.7 copy-done.11
  12.4 0.0 copy-start.12
  12.4 0.7 copy-done.12
  13.0 0.0 copy-start.13
  13.0 0.7 copy-done.13
  13.7 0.0 copy-start.14
  13.7 0.7 copy-done.14
  14.4 96.8 %vcycle.1 = f32[32,64,128]{2,1,0:T(8,128)S(1)} custom-call(bf16[32,64,128]{2,1,0:T(8,128)(2,1)S(1)} %copy-done.2, bf16[128,1024]{1,0:T(8,128)(2,1)S(1)} %copy-done.3, s32[32,3]{1,0:T(8,128)S(1)} %copy.18.refs_2_, bf16[32,384,128]{2,1,0:T(8,128)(2,1)S(1)} %bitcast.3, f32[32,128]{1,0:T(8,128)S(1)} %copy-done.5, s32[32,128]{1,0:T(8,128)S(1)} %copy-done.6, ...), custom_call_target="tpu_custom_call" | custom-call | tf_op jit(solution)/shard_map/vcycle/pallas_call | solution.py:569
  111.2 1.0 copy.21
Async XLA Ops:
  1.5 1.9 %copy-start = (bf16[32,3,128,128]{3,2,1,0:T(8,128)(2,1)S(1)}, bf16[32,3,128,128]{3,2,1,0:T(8,128)(2,1)}, u32[]{:S(2)}) copy-start(bf16[32,3,128,128]{3,2,1,0:T(8,128)(2,1)} %param.18) | copy-start | bytes 9437188
  3.4 1.1 %copy-start.1 = (bf16[8,3,128,128]{3,2,1,0:T(8,128)(2,1)S(1)}, bf16[8,3,128,128]{3,2,1,0:T(8,128)(2,1)}, u32[]{:S(2)}) copy-start(bf16[8,3,128,128]{3,2,1,0:T(8,128)(2,1)} %param.23) | copy-start | bytes 2359300
  4.5 1.0 copy-start.2
  5.6 0.9 copy-start.3
  6.5 0.9 copy-start.4
  7.5 0.7 copy-start.5
  8.2 0.7 copy-start.6
  8.9 0.7 copy-start.7
  9.6 0.7 copy-start.8
  10.3 0.7 copy-start.9
  11.0 0.7 copy-start.10
  11.7 0.7 copy-start.11
  12.4 0.7 copy-start.12
  13.0 0.7 copy-start.13
  13.7 0.7 copy-start.14
where the time goes:
time: 113 us; the launch traced here: 112 us
  Pallas kernels  96.8 us (86%)
  local copies, waits for them, and re-layouts  15.4 us (14%)
    pallas_call x1, Pallas kernels, on_device(): pl.pallas_call(functools.partial(kernel, sizes, r, bs, k, m3), out_shape=...  96.8 us
    unnamed x33, local copies, waits for them, and re-layouts  15.4 us

commit v1 on v0

--- a/solution.py
+++ b/solution.py
@@ -73,6 +73,9 @@
 
     def inner(self):
         return (0, 0) if self.single else (2, self.n - 2)
+
+    def column(self, b, k):
+        return self.columns[b, k] if self.single else self.columns[k, b]
 
     def weight_sums(self, b):
         w = self.ref["w"][b]
@@ -100,7 +103,7 @@
             buf, offset = self.ref[f"hi{i}"], self.base + self.n - 4
         top = buf.shape[0] - 1
         picked = [
-            buf[jnp.clip(self.columns[b, k] - offset, 0, top)] for k in range(self.k)
+            buf[jnp.clip(self.column(b, k) - offset, 0, top)] for k in range(self.k)
         ]
         left = jnp.concatenate(picked, axis=1)
         return jnp.dot(left, self.ref["w"][b], preferred_element_type=F32) * self.scale
@@ -362,14 +365,15 @@
     refs = list(refs)
     take = lambda count: [refs.pop(0) for _ in range(count)]
     rhs_hbm, inverse_hbm = take(2)
-    columns, hbm = [], []
+    columns_hbm, hbm = [], []
     for _ in sizes:
-        columns.append(refs.pop(0))
+        columns_hbm.append(refs.pop(0))
         hbm.append(dict(zip(LEVEL_HBM, take(4))))
-    (out_hbm,) = take(1)
+    (out,) = take(1)
     scratch = [dict(zip(LEVEL_SCRATCH, take(len(LEVEL_SCRATCH)))) for _ in sizes]
-    rhs, f_second, f_third, inverse, gathered, out = take(6)
-    send, recv, gather_send, gather_recv, local, out_sem = take(6)
+    columns = take(len(sizes))
+    rhs, f_second, f_third, inverse, gathered = take(5)
+    send, recv, gather_send, gather_recv, local = take(5)
 
     ops = Ops(send, recv)
     levels = []
@@ -394,6 +398,8 @@
         early.append(load(hbm[0]["w"].at[at], scratch[0]["w"].at[at]))
     early.append(load(hbm[0]["deg"], scratch[0]["deg"]))
     early.append(load(rhs_hbm, rhs))
+    for src, dst in zip(columns_hbm, columns):
+        early.append(load(src, dst))
     middle = load(hbm[0]["w"].at[2 : n - 2], scratch[0]["w"].at[2 : n - 2])
     later = [
         load(hbm[0][name], scratch[0][name]) for name in ("own", "slot")
@@ -425,14 +431,12 @@
     made = [fine.weight_sums(b) for b in fine.edges()]
     for b, total in zip(fine.edges(), made):
         diagonal_and_start(b, total)
+    middle.wait()
+    grouped(*fine.inner(), fine.weight_sums, diagonal_and_start)
     pl.semaphore_wait(
         barrier, ops.cols - 1 + next_row.astype(jnp.int32) + previous_row.astype(jnp.int32)
     )
-
     fine.ops.start(fine.halo_copies(0))
-    middle.wait()
-
-    grouped(*fine.inner(), fine.weight_sums, diagonal_and_start)
     for copy in later:
         copy.wait()
     loop(0, fine.n // 2, fine.make_onehot, 1)
@@ -499,13 +503,10 @@
         out[b] = x
 
     fine.up(put_out)
-    result = pltpu.make_async_copy(out, out_hbm, out_sem.at[0])
-    result.start()
     for level in levels:
         level.drain()
     for copy in sends:
         copy.wait_send()
-    result.wait()
 
 
 def on_device(
@@ -523,15 +524,14 @@
     sizes = ((n0, n1 * bs), (n1, n2 * bs), (n2, c3))
     merged = lambda w: w.reshape(w.shape[0], k * bs, bs)
     args = [right_sides, coarse_inverse]
-    specs = [pl.BlockSpec(memory_space=pl.ANY)] * 2
+    specs = [pl.BlockSpec(memory_space=pltpu.HBM)] * 2
     for w, c, d, o, s in (
         (weights_fine, columns_fine, degree_fine, owners_fine, slots_fine),
         (weights_second, columns_second, degree_second, owners_second, slots_second),
         (weights_third, columns_third, degree_third, owners_third, slots_third),
     ):
-        args += [c, merged(w), d, o, s]
-        specs += [pl.BlockSpec(memory_space=pltpu.SMEM)]
-        specs += [pl.BlockSpec(memory_space=pl.ANY)] * 4
+        args += [c.T if c.shape[0] >= 4 else c, merged(w), d, o, s]
+        specs += [pl.BlockSpec(memory_space=pltpu.HBM)] * 5
     scratch = []
     for n, t in sizes:
         scratch += [
@@ -553,30 +553,31 @@
             pltpu.VMEM((2, r, t), BF16),
         ]
     scratch += [
+        pltpu.SMEM((k, n0), jnp.int32),
+        pltpu.SMEM((k, n1), jnp.int32),
+        pltpu.SMEM((n2, k), jnp.int32),
         pltpu.VMEM((n0, r, bs), BF16),
         pltpu.VMEM((n1, r, bs), F32),
         pltpu.VMEM((n2, r, bs), F32),
         pltpu.VMEM((c3, m3), BF16),
         pltpu.VMEM((cols, r, c3), BF16),
-        pltpu.VMEM((n0, r, bs), F32),
         pltpu.SemaphoreType.DMA((18, 2)),
         pltpu.SemaphoreType.DMA((18, 2)),
         pltpu.SemaphoreType.DMA((cols,)),
         pltpu.SemaphoreType.DMA((cols,)),
         pltpu.SemaphoreType.DMA((24,)),
-        pltpu.SemaphoreType.DMA((1,)),
     ]
     return pl.pallas_call(
         functools.partial(kernel, sizes, r, bs, k, m3),
         out_shape=jax.ShapeDtypeStruct((n0, r, bs), F32),
         in_specs=specs,
-        out_specs=pl.BlockSpec(memory_space=pl.ANY),
+        out_specs=pl.BlockSpec(memory_space=pltpu.VMEM),
         scratch_shapes=scratch,
         compiler_params=pltpu.CompilerParams(
             collective_id=0, has_side_effects=True, vmem_limit_bytes=48 * 1024 * 1024
         ),
         name="vcycle",
-    )(*args)
+    )(*[pltpu.with_memory_space_constraint(a, pltpu.HBM) for a in args])
 
 
 def solution(mesh):

time: 113 us -> 98 us (0.87)
  local copies, waits for them, and re-layouts: 15.4 us -> 0.97 us
    unnamed x33 -> x1, local copies, waits for them, and re-layouts: 15.4 us -> 0.97 us
where the time goes in v1:
time: 98 us; the launch traced here: 97.8 us
  Pallas kernels  96.8 us (99%)
    pallas_call x1, Pallas kernels, on_device(): pl.pallas_call(functools.partial(kernel, sizes, r, bs, k, m3), out_shape=...  96.8 us

profile of v1, /device:TPU:3, one launch (start us, length us, event | category | flops | bytes accessed | tf_op | source)
XLA Modules:
  0.0 97.8 jit_solution(7605129986520938586)
XLA Ops:
  0.0 96.8 %vcycle.1 = f32[32,64,128]{2,1,0:T(8,128)S(1)} custom-call(bf16[32,64,128]{2,1,0:T(8,128)(2,1)} %refs_0_.1, bf16[128,1024]{1,0:T(8,128)(2,1)} %refs_1_.1, s32[3,32]{1,0:T(4,128)} %bitcast.8, bf16[32,384,128]{2,1,0:T(8,128)(2,1)} %bitcast.5, f32[32,128]{1,0:T(8,128)} %refs_4_.1, s32[32,128]{1,0:T(8,128)} %refs_5_.1, s32[32,128]{1,0:T(8,128)} %refs_6_.1, ...), custom_call_target="tpu_custom_call" | custom-call | tf_op jit(solution)/shard_map/vcycle/pallas_call | solution.py:570
  96.8 1.0 copy.19

commit v2 on v1

v2 whole, which is shorter than its diff:
```python
import functools

import jax
import jax.numpy as jnp
from jax import lax
from jax.experimental import pallas as pl
from jax.experimental.pallas import tpu as pltpu
from jax.sharding import PartitionSpec as P

F32 = jnp.float32
BF16 = jnp.bfloat16
MESH = pl.DeviceIdType.MESH
DAMPING = 0.8


def loop(low, high, body, unroll=4):
    count = high - low
    if count <= 0:
        return
    while count % unroll:
        unroll -= 1

    if count == unroll:
        for inner in range(count):
            body(low + inner)
        return

    def step(outer, carry):
        for inner in range(unroll):
            body(low + outer * unroll + inner)
        return carry

    lax.fori_loop(0, count // unroll, step, 0)


def grouped(low, high, first, then, unroll=7):
    count = high - low
    if count <= 0:
        return
    while count % unroll:
        unroll -= 1

    def group(start):
        made = [first(start + inner) for inner in range(unroll)]
        for inner in range(unroll):
            then(start + inner, made[inner])

    if count == unroll:
        group(low)
        return

    def step(outer, carry):
        group(low + outer * unroll)
        return carry

    lax.fori_loop(0, count // unroll, step, 0)


class Copy:
    def __init__(self, ops, descriptor, delta):
        self.ops, self.descriptor, self.delta = ops, descriptor, delta

    def start(self):
        pl.when(self.ops.has(self.delta))(lambda: self.descriptor.start())

    def wait(self):
        pl.when(self.ops.has(-self.delta))(lambda: self.descriptor.wait_recv())

    def drain(self):
        pl.when(self.ops.has(self.delta))(lambda: self.descriptor.wait_send())


def start(copies):
    for copy in copies:
        copy.start()


def wait(copies):
    for copy in copies:
        copy.wait()


class Ops:
    def __init__(self, send, recv):
        self.send, self.recv = send, recv
        self.rows, self.cols = lax.axis_size("row"), lax.axis_size("col")
        self.total = self.rows * self.cols
        self.row, self.col = lax.axis_index("row"), lax.axis_index("col")
        self.me = self.row * self.cols + self.col
        self.copies = []

    def has(self, delta):
        return self.me < self.total - delta if delta > 0 else self.me >= -delta

    def peer(self, delta):
        index = jnp.clip(self.me + delta, 0, self.total - 1)
        return (index // self.cols, index % self.cols)

    def across(self, delta):
        over = self.col + delta >= self.cols if delta > 0 else self.col + delta < 0
        return jnp.logical_and(self.has(delta), over)

    def copy(self, src, dst, delta):
        slot = len(self.copies)
        descriptor = pltpu.make_async_remote_copy(
            src, dst, self.send.at[slot], self.recv.at[slot],
            device_id=self.peer(delta), device_id_type=MESH,
        )
        self.copies.append(Copy(self, descriptor, delta))
        return self.copies[-1]


class Level:
    def __init__(self, n, t, r, bs, k, ref, columns, ops):
        self.n, self.t, self.r, self.bs, self.k = n, t, r, bs, k
        self.ref, self.columns, self.ops = ref, columns, ops
        self.base = ops.me * n
        self.scale = 1.0 / (k * bs)

    def weight_sums(self, b):
        w = self.ref["w"][b]
        return jnp.dot(jnp.ones((8, w.shape[0]), BF16), w, preferred_element_type=F32)

    def put_diagonal(self, b, total):
        degree = self.ref["deg"][pl.ds(b, 1), :]
        g = degree + total * self.scale
        self.ref["g"][b] = g
        self.ref["gi"][b] = DAMPING / g

    def spread(self, row):
        return jnp.broadcast_to(row, (self.r, self.bs))

    def hot(self, row):
        slots = jnp.broadcast_to(row, (self.t, self.bs))
        index = lax.broadcasted_iota(jnp.int32, (self.t, self.bs), 0)
        return jnp.where(index == slots, 1.0, 0.0).astype(BF16)

    def put_residual(self, columns, res, rel):
        rows = self.r
        out = self.ref["res"]
        zero = jnp.zeros_like(res)
        out[0:rows, columns] = jnp.where(rel < 0, res, zero).astype(BF16)
        out[rows : 2 * rows, columns] = jnp.where(rel == 0, res, zero).astype(BF16)
        out[2 * rows : 3 * rows, columns] = jnp.where(rel > 0, res, zero).astype(BF16)

    def restricted(self, res, hot):
        return lax.dot_general(
            res, hot, (((1,), (1,)), ((), ())), preferred_element_type=F32
        )


class Fine(Level):
    def __init__(self, *args):
        super().__init__(*args)
        ref, ops, n = self.ref, self.ops, self.n
        self.halo = []
        for i in range(4):
            vb = ref[f"vb{i}"]
            self.halo.append([
                ops.copy(vb.at[n - 2 : n], ref[f"lo{i}"].at[0:2], 1),
                ops.copy(vb.at[0:2], ref[f"hi{i}"].at[4:6], -1),
            ])
        self.prolong = [
            ops.copy(ref["uout"], ref["uin"].at[0], 1),
            ops.copy(ref["uout"], ref["uin"].at[1], -1),
        ]
        out, got = ref["rout"], ref["rin"]
        tiles = self.t // (2 * self.bs)
        last = tiles - 1
        self.tiles = [0, last] + list(range(1, last))
        self.restrict_copies = {}
        for j in self.tiles:
            at = slice(2 * j, 2 * j + 2)
            made = [
                ops.copy(out.at[2, at], got.at[0, at], 1),
                ops.copy(out.at[0, at], got.at[1, at], -1),
            ]
            if j == 0:
                made.append(ops.copy(out.at[1, at], ref["near"].at[1], -1))
                made.append(ops.copy(out.at[0, at], ref["far"].at[1], -2))
            if j == last:
                made.append(ops.copy(out.at[1, at], ref["near"].at[0], 1))
                made.append(ops.copy(out.at[2, at], ref["far"].at[0], 2))
            self.restrict_copies[j] = made

    def edges(self):
        return [0, 1, self.n - 2, self.n - 1]

    def inner(self):
        return 2, self.n - 2

    def row(self, name, b):
        return self.spread(self.ref[name][b, 0:1, :])

    def f(self, b):
        return self.ref["f"][b].astype(F32)

    def product(self, i, b, where):
        if where == "inner":
            buf, offset = self.ref[f"vb{i}"], self.base
        elif where == "low":
            buf, offset = self.ref[f"lo{i}"], self.base - 2
        else:
            buf, offset = self.ref[f"hi{i}"], self.base + self.n - 4
        top = buf.shape[0] - 1
        picked = [
            buf[jnp.clip(self.columns[k, b] - offset, 0, top)] for k in range(self.k)
        ]
        left = jnp.concatenate(picked, axis=1)
        return jnp.dot(left, self.ref["w"][b], preferred_element_type=F32) * self.scale

    def apply(self, i, body):
        grouped(*self.inner(), lambda b: self.product(i, b, "inner"), body)
        n = self.n
        self.ref[f"lo{i}"][2:6] = self.ref[f"vb{i}"][0:4]
        self.ref[f"hi{i}"][0:4] = self.ref[f"vb{i}"][n - 4 : n]
        wait(self.halo[i])
        made = [self.product(i, b, "low" if b < 2 else "high") for b in self.edges()]
        for b, product in zip(self.edges(), made):
            body(b, product)

    def start_block(self, b):
        self.ref["vb0"][b] = (self.row("gi", b) * self.f(b)).astype(BF16)

    def first_sweep(self, b, product):
        f, gi = self.f(b), self.row("gi", b)
        x0 = gi * f
        x = (1.0 - DAMPING) * x0 + gi * (f + product)
        self.ref["x"][b] = x
        self.ref["vb1"][b] = x.astype(BF16)

    def at(self, b):
        return pl.ds(pl.multiple_of(b * self.bs, self.bs), self.bs)

    def owner(self, b):
        return self.spread(self.ref["own"][pl.ds(b, 1), :] - self.ops.me)

    def residual(self, b, product):
        res = self.f(b) - self.row("g", b) * self.ref["x"][b] + product
        self.put_residual(self.at(b), res, self.owner(b))

    def make_onehot(self, b):
        self.ref["oh"][:, self.at(b)] = self.hot(self.ref["slot"][pl.ds(b, 1), :])

    def restrict(self):
        r, bs = self.r, self.bs
        for j in self.tiles:
            at = slice(2 * j * bs, (2 * j + 2) * bs)
            value = self.restricted(self.ref["res"][...], self.ref["oh"][at, :])
            for half in range(2):
                b = 2 * j + half
                part = value[:, half * bs : (half + 1) * bs]
                for way in range(3):
                    self.ref["rout"][way, b] = part[way * r : (way + 1) * r].astype(BF16)
                self.ref["rown"][b] = part[r : 2 * r]
            start(self.restrict_copies[j])

    def received(self, below):
        for j in self.tiles:
            wait(self.restrict_copies[j])
        got, out = self.ref["rin"], self.ref["rout"]
        n = below.n
        for b in range(n):
            below.ref["f"][b] = self.ref["rown"][b] + got[0, b].astype(F32) + got[1, b].astype(F32)
        for side, way, first in ((0, 0, n - 2), (1, 2, 0)):
            for j in range(2):
                below.ref["fn"][side, j] = (
                    self.ref["near"][side, j].astype(F32)
                    + self.ref["far"][side, j].astype(F32)
                    + out[way, first + j].astype(F32)
                )

    def pair_columns(self, pair):
        return pl.ds(pl.multiple_of(pair * 2 * self.bs, 2 * self.bs), 2 * self.bs)

    def own_part(self, pair):
        return jnp.dot(
            self.ref["uout"][...], self.ref["oh"][:, self.pair_columns(pair)],
            preferred_element_type=F32,
        )

    def add_own(self, pair, value):
        for half in range(2):
            b = 2 * pair + half
            part = value[:, half * self.bs : (half + 1) * self.bs]
            self.ref["x"][b] = self.ref["x"][b] + jnp.where(self.owner(b) == 0, part, 0.0)

    def others_part(self, pair):
        left = jnp.concatenate([self.ref["uin"][0], self.ref["uin"][1]], axis=0)
        return jnp.dot(
            left, self.ref["oh"][:, self.pair_columns(pair)], preferred_element_type=F32
        )

    def add_others(self, pair, value):
        for half in range(2):
            b = 2 * pair + half
            at = slice(half * self.bs, (half + 1) * self.bs)
            rel = self.owner(b)
            x = self.ref["x"][b]
            x = x + jnp.where(rel < 0, value[0 : self.r, at], 0.0)
            x = x + jnp.where(rel > 0, value[self.r : 2 * self.r, at], 0.0)
            self.ref["x"][b] = x
            self.ref["vb2"][b] = x.astype(BF16)

    def sweep(self, i, out):
        def body(b, product):
            x = (1.0 - DAMPING) * self.ref["x"][b] + self.row("gi", b) * (self.f(b) + product)
            if out is None:
                self.ref["x"][b] = x
                self.ref[f"vb{i + 1}"][b] = x.astype(BF16)
            else:
                out[b] = x

        return body

    def up(self, out):
        start(self.prolong)
        pairs = self.n // 2
        grouped(0, pairs, self.own_part, self.add_own, 2)
        wait(self.prolong)
        ends = [0, pairs - 1]
        made = [self.others_part(pair) for pair in ends]
        for pair, value in zip(ends, made):
            self.add_others(pair, value)
        start(self.halo[2])
        grouped(1, pairs - 1, self.others_part, self.add_others, 2)
        self.apply(2, self.sweep(2, None))
        start(self.halo[3])
        self.apply(3, self.sweep(3, out))

    def clear_ends(self):
        for name, low, high in (("rin", 0, 1), ("uin", 0, 1), ("near", 0, 1), ("far", 0, 1)):
            ref = self.ref[name]
            for entry, missing in ((low, -2 if name == "far" else -1), (high, 2 if name == "far" else 1)):

                @pl.when(jnp.logical_not(self.ops.has(missing)))
                def _():
                    ref[entry] = jnp.zeros(ref.shape[1:], ref.dtype)


class Small(Level):
    def __init__(self, n, t, r, bs, k, ref, columns, ops, halo, weight_ways, degree_ways, send_ways):
        super().__init__(n, t, r, bs, k, ref, columns[0], ops)
        self.halo, self.m = halo, min(n, 2)
        self.other_columns = columns[1:]
        self.weight_ways, self.degree_ways, self.send_ways = weight_ways, degree_ways, send_ways
        ways = weight_ways
        self.tables, self.weights = [], []
        for at, d in enumerate(ways):
            self.tables.append(ops.copy(ref["own"], ref["ownn"].at[at], -d))
            self.tables.append(ops.copy(ref["slot"], ref["slotn"].at[at], -d))
            self.tables.append(ops.copy(columns[0], columns[1 + at], -d))
        for at, d in enumerate(degree_ways):
            self.tables.append(ops.copy(ref["g"].at[self.edge(d)], ref["gn"].at[at], -d))
        for j in range(self.m):
            for rows in range(k):
                part = slice(rows * bs, (rows + 1) * bs)
                group = []
                for at, d in enumerate(ways):
                    source = self.edge(d).start + j
                    group.append(ops.copy(ref["w"].at[source, part], ref["wn"].at[at, j, part], -d))
                self.weights.append(group)
        self.sends = [
            ops.copy(ref["uout"], ref["uin"].at[at], -d) for at, d in enumerate(send_ways)
        ]

    def edge(self, d):
        return slice(self.n - self.m, self.n) if d < 0 else slice(0, self.m)

    def place(self, b):
        d = b // self.n
        j = b - d * self.n
        return d, j, j - self.edge(d).start

    def column(self, b, k):
        d, j, _ = self.place(b)
        table = self.columns if d == 0 else self.other_columns[self.weight_ways.index(d)]
        return table[j, k] if self.n < 4 else table[k, j]

    def w(self, b):
        d, j, e = self.place(b)
        return self.ref["w"][j] if d == 0 else self.ref["wn"][self.weight_ways.index(d), e]

    def row(self, name, b):
        d, j, e = self.place(b)
        if d == 0:
            return self.spread(self.ref[name][j, 0:1, :])
        return self.spread(self.ref[name + "n"][self.degree_ways.index(d), e, 0:1, :])

    def f(self, b):
        d, j, e = self.place(b)
        if d == 0:
            return self.ref["f"][j]
        return self.ref["fn"][self.degree_ways.index(d), e].astype(F32)

    def table(self, name, b):
        d, j, _ = self.place(b)
        if d == 0:
            return self.ref[name][j : j + 1, :]
        return self.ref[name + "n"][self.weight_ways.index(d), j : j + 1, :]

    def owner(self, b):
        return self.spread(self.table("own", b) - self.ops.me)

    def invert(self):
        for at in range(len(self.degree_ways)):
            for e in range(self.m):
                self.ref["gin"][at, e] = DAMPING / self.ref["gn"][at, e]

    def make_onehots(self, reach):
        for b in range(-reach, self.n + reach):
            at = (b + reach) * self.bs
            self.ref["oh"][:, at : at + self.bs] = self.hot(self.table("slot", b))

    def product(self, i, b):
        buf = self.ref[f"vb{i}"]
        offset = self.base - self.halo
        top = buf.shape[0] - 1
        picked = [
            buf[jnp.clip(self.column(b, k) - offset, 0, top)] for k in range(self.k)
        ]
        left = jnp.concatenate(picked, axis=1)
        return jnp.dot(left, self.w(b), preferred_element_type=F32) * self.scale

    def apply(self, i, blocks, body, size=6):
        blocks = list(blocks)
        for low in range(0, len(blocks), size):
            group = blocks[low : low + size]
            made = [self.product(i, b) for b in group]
            for b, product in zip(group, made):
                body(b, product)

    def start_blocks(self, low, high):
        for b in range(low, high):
            self.ref["vb0"][b + self.halo] = (self.row("gi", b) * self.f(b)).astype(BF16)

    def first_sweep(self, b, product):
        f, gi = self.f(b), self.row("gi", b)
        x0 = gi * f
        x = (1.0 - DAMPING) * x0 + gi * (f + product)
        self.ref["x"][b + self.halo] = x
        self.ref["vb1"][b + self.halo] = x.astype(BF16)

    def residual_of(self, b, product):
        return self.f(b) - self.row("g", b) * self.ref["x"][b + self.halo] + product

    def add_correction(self, reach):
        bs, r = self.bs, self.r
        corrections = {0: self.ref["uout"]}
        for at, d in enumerate(self.send_ways):
            corrections[d] = self.ref["uin"].at[at]
        for b in range(-reach, self.n + reach, 2):
            d, _, _ = self.place(b)
            left = jnp.concatenate([corrections[d + way][...] for way in (-1, 0, 1)], axis=0)
            at = (b + reach) * bs
            value = jnp.dot(left, self.ref["oh"][:, at : at + 2 * bs], preferred_element_type=F32)
            for half in range(2):
                part = value[:, half * bs : (half + 1) * bs]
                rel = self.owner(b + half) - d
                low, own, high = (part[way * r : (way + 1) * r] for way in range(3))
                add = jnp.where(rel == 0, own, jnp.where(rel < 0, low, high))
                x = self.ref["x"][b + half + self.halo] + add
                self.ref["x"][b + half + self.halo] = x
                self.ref["vb2"][b + half + self.halo] = x.astype(BF16)

    def sweep(self, i, out=None):
        def body(b, product):
            h = self.halo
            x = (1.0 - DAMPING) * self.ref["x"][b + h] + self.row("gi", b) * (self.f(b) + product)
            if out is None:
                self.ref["x"][b + h] = x
                self.ref[f"vb{i + 1}"][b + h] = x.astype(BF16)
            else:
                out(b, x)

        return body

    def up(self, out):
        start(self.sends)
        return self.sends

    def clear_ends(self):
        for at, d in enumerate(self.weight_ways):

            @pl.when(jnp.logical_not(self.ops.has(d)))
            def _():
                self.ref["ownn"][at] = jnp.full(self.ref["ownn"].shape[1:], -8, jnp.int32)
                self.ref["slotn"][at] = jnp.zeros(self.ref["slotn"].shape[1:], jnp.int32)
                self.ref["wn"][at] = jnp.zeros(self.ref["wn"].shape[1:], BF16)
                columns = self.other_columns[at]
                for i in range(columns.shape[0]):
                    for j in range(columns.shape[1]):
                        columns[i, j] = 0

        for at, d in enumerate(self.degree_ways):

            @pl.when(jnp.logical_not(self.ops.has(d)))
            def _():
                self.ref["gn"][at] = jnp.ones(self.ref["gn"].shape[1:], F32)
                self.ref["fn"][at] = jnp.zeros(self.ref["fn"].shape[1:], self.ref["fn"].dtype)

        for at, d in enumerate(self.send_ways):

            @pl.when(jnp.logical_not(self.ops.has(d)))
            def _():
                self.ref["uin"][at] = jnp.zeros(self.ref["uin"].shape[1:], BF16)


class Second(Small):
    def __init__(self, *args):
        super().__init__(*args, 4, (-1, 1), (-1, 1), (-2, -1, 1, 2))
        ref, ops, n, h = self.ref, self.ops, self.n, self.halo
        vb, got = ref["vb1"], ref["vin"]
        own = lambda low, high: vb.at[h + low : h + high]
        self.halo_near = [
            ops.copy(own(n - 2, n), got.at[0, 2:4], 1), ops.copy(own(0, 2), got.at[1, 0:2], -1)
        ]
        self.halo_far = [
            ops.copy(own(n - 4, n - 2), got.at[0, 0:2], 1), ops.copy(own(2, 4), got.at[1, 2:4], -1)
        ]
        self.restrict_copies = [
            ops.copy(ref["rout"].at[1], ref["rin"].at[0], 1),
            ops.copy(ref["rout"].at[0], ref["rin"].at[1], -1),
        ]

    def residual(self, b, product):
        at = slice(b * self.bs, (b + 1) * self.bs)
        self.put_residual(at, self.residual_of(b, product), self.owner(b))

    def down(self, below, meanwhile):
        n, h, r, bs = self.n, self.halo, self.r, self.bs
        self.start_blocks(-2, n + 2)
        edges = [0, 1, n - 2, n - 1]
        self.apply(0, edges, self.first_sweep)
        start(self.halo_near)
        self.apply(0, range(2, n - 2), self.first_sweep)
        start(self.halo_far)
        meanwhile()
        self.apply(1, range(2, n - 2), self.residual)
        wait(self.halo_near)
        self.ref["vb1"][h - 2 : h] = self.ref["vin"][0, 2:4]
        self.ref["vb1"][h + n : h + n + 2] = self.ref["vin"][1, 0:2]
        self.apply(1, edges, self.residual)
        reach = 4
        own = slice(reach * bs, (reach + n) * bs)
        value = self.restricted(self.ref["res"][...], self.ref["oh"][:, own])
        for b in range(below.n):
            at = slice(b * bs, (b + 1) * bs)
            self.ref["rout"][0, b] = value[0:r, at].astype(BF16)
            self.ref["rout"][1, b] = value[2 * r : 3 * r, at].astype(BF16)
        start(self.restrict_copies)
        for b in range(below.n):
            self.ref["rown"][b] = value[r : 2 * r, b * bs : (b + 1) * bs]

    def received(self, below):
        wait(self.restrict_copies)
        got = self.ref["rin"]
        for b in range(below.n):
            f = self.ref["rown"][b] + got[0, b].astype(F32) + got[1, b].astype(F32)
            below.ref["f"][b] = f
            below.ref["fout"][b] = f.astype(BF16)

    def finish(self, out):
        n, h = self.n, self.halo
        wait(self.halo_far)
        for j in range(4):
            self.ref["x"][h - 4 + j] = self.ref["vin"][0, j].astype(F32)
            self.ref["x"][h + n + j] = self.ref["vin"][1, j].astype(F32)
        wait(self.sends)
        self.add_correction(4)
        for group in self.weights:
            wait(group)
        self.apply(2, range(-2, n + 2), self.sweep(2))
        self.apply(3, range(n), self.sweep(3, out))

    def clear_ends(self):
        super().clear_ends()
        for name in ("rin", "vin"):
            for at, d in ((0, -1), (1, 1)):

                @pl.when(jnp.logical_not(self.ops.has(d)))
                def _():
                    self.ref[name][at] = jnp.zeros(self.ref[name].shape[1:], BF16)


class Third(Small):
    def __init__(self, *args):
        super().__init__(*args, 6, (-2, -1, 1, 2), (-3, -2, -1, 1, 2, 3), (-3, -2, -1, 1, 2, 3))
        ref, ops = self.ref, self.ops
        self.sources = [
            ops.copy(ref["fout"], ref["fn"].at[at], -d) for at, d in enumerate(self.degree_ways)
        ]

    def down(self, into):
        n, bs = self.n, self.bs
        wait(self.sources)
        self.start_blocks(-6, n + 6)
        for group in self.weights:
            wait(group)
        self.apply(0, range(-4, n + 4), self.first_sweep)

        def residual(b, product):
            res = self.residual_of(b, product)
            at = (b + 2) * bs
            kept = jnp.where(self.owner(b) == 0, res, jnp.zeros_like(res))
            self.ref["res"][:, at : at + bs] = kept.astype(BF16)

        self.apply(1, range(-2, n + 2), residual)
        near = slice(2 * bs, (n + 6) * bs)
        into(self.restricted(self.ref["res"][...], self.ref["oh"][:, near]))

    def finish(self, out):
        n = self.n
        wait(self.sends)
        self.add_correction(4)
        self.apply(2, range(-2, n + 2), self.sweep(2))
        self.apply(3, range(n), self.sweep(3, out))


LEVEL_HBM = ("w", "deg", "own", "slot")
SHARED = ("w", "deg", "own", "slot", "g", "gi", "x", "vb0", "vb1", "vb2", "vb3", "res", "oh", "uout", "uin")
FINE = SHARED + (
    "lo0", "lo1", "lo2", "lo3", "hi0", "hi1", "hi2", "hi3", "rout", "rin", "rown", "near", "far",
)
SMALL = SHARED + ("f", "fn", "wn", "ownn", "slotn", "gn", "gin")
SECOND = SMALL + ("rout", "rin", "rown", "vin")
THIRD = SMALL + ("fout",)


def kernel(sizes, rhs_count, bs, k, *refs):
    refs = list(refs)
    take = lambda count: [refs.pop(0) for _ in range(count)]
    rhs_hbm, inverse_hbm = take(2)
    columns_hbm, hbm = [], []
    for _ in sizes:
        columns_hbm.append(refs.pop(0))
        hbm.append(dict(zip(LEVEL_HBM, take(4))))
    (out,) = take(1)
    scratch = [dict(zip(names, take(len(names)))) for names in (FINE, SECOND, THIRD)]
    columns = [take(1), take(3), take(5)]
    rhs, inverse, gathered = take(3)
    send, recv, gather_send, gather_recv, local = take(5)

    ops = Ops(send, recv)
    scratch[0]["f"] = rhs
    (n0, t0), (n1, t1), (n2, t2) = sizes
    fine = Fine(n0, t0, rhs_count, bs, k, scratch[0], columns[0][0], ops)
    second = Second(n1, t1, rhs_count, bs, k, scratch[1], columns[1], ops)
    third = Third(n2, t2, rhs_count, bs, k, scratch[2], columns[2], ops)
    levels = [fine, second, third]

    loads = []

    def load(src, dst):
        copy = pltpu.make_async_copy(src, dst, local.at[len(loads)])
        loads.append(copy)
        copy.start()
        return copy

    n = fine.n
    early = []
    for at in (slice(0, 2), slice(n - 2, n)):
        early.append(load(hbm[0]["w"].at[at], scratch[0]["w"].at[at]))
    early.append(load(hbm[0]["deg"], scratch[0]["deg"]))
    early.append(load(rhs_hbm, rhs))
    for level in range(3):
        early.append(load(columns_hbm[level], columns[level][0]))
    middle = load(hbm[0]["w"].at[2 : n - 2], scratch[0]["w"].at[2 : n - 2])
    later = [load(hbm[0][name], scratch[0][name]) for name in ("own", "slot")]
    for position in (1, 2):
        later += [load(hbm[position][name], scratch[position][name]) for name in LEVEL_HBM]
    last = load(inverse_hbm, inverse)

    barrier = pltpu.get_barrier_semaphore()
    expected = ops.cols - 1
    for delta in (-3, -2, -1, 1, 2, 3):
        outside = ops.across(delta)
        pl.when(outside)(
            lambda: pl.semaphore_signal(
                barrier, inc=1, device_id=ops.peer(delta), device_id_type=MESH
            )
        )
        expected = expected + outside.astype(jnp.int32)
    for step in range(1, ops.cols):
        peer = lax.rem(ops.col + step, ops.cols)
        pl.semaphore_signal(barrier, inc=1, device_id=(ops.row, peer), device_id_type=MESH)
    for level in levels:
        level.clear_ends()
    for copy in early:
        copy.wait()

    def diagonal_and_start(b, total):
        fine.put_diagonal(b, total)
        fine.start_block(b)

    made = [fine.weight_sums(b) for b in fine.edges()]
    for b, total in zip(fine.edges(), made):
        diagonal_and_start(b, total)
    middle.wait()
    grouped(*fine.inner(), fine.weight_sums, diagonal_and_start)
    for copy in later:
        copy.wait()
    for level in (second, third):
        grouped(0, level.n, level.weight_sums, level.put_diagonal, 8)
    pl.semaphore_wait(barrier, expected)

    start(fine.halo[0])
    start(second.tables)
    start(third.tables)
    third_weights = list(third.weights)
    for _ in range(2):
        start(third_weights.pop(0))
    loop(0, n // 2, fine.make_onehot, 1)
    fine.apply(0, fine.first_sweep)
    start(fine.halo[1])
    for _ in range(2):
        start(third_weights.pop(0))
    loop(n // 2, n, fine.make_onehot, 1)
    fine.apply(1, fine.residual)
    fine.restrict()
    for level in (second, third):
        wait(level.tables)
        level.invert()
        level.make_onehots(4)
    fine.received(second)

    def rest_of_weights():
        while third_weights:
            start(third_weights.pop(0))

    second.down(third, rest_of_weights)
    second_weights = list(second.weights)
    for _ in range(2):
        start(second_weights.pop(0))
    second.received(third)
    start(third.sources)
    for _ in range(2):
        start(second_weights.pop(0))

    def into_coarse(value):
        gathered[ops.col] = value.astype(BF16)

    third.down(into_coarse)

    sends = []
    for step in range(1, ops.cols):
        peer = lax.rem(ops.col + step, ops.cols)
        copy = pltpu.make_async_remote_copy(
            gathered.at[ops.col], gathered.at[ops.col],
            gather_send.at[step - 1], gather_recv.at[step - 1],
            device_id=(ops.row, peer), device_id_type=MESH,
        )
        copy.start()
        sends.append(copy)
    last.wait()
    for step in range(1, ops.cols):
        source = lax.rem(ops.col + ops.cols - step, ops.cols)
        pltpu.make_async_remote_copy(
            gathered.at[source], gathered.at[source],
            gather_send.at[step - 1], gather_recv.at[step - 1],
            device_id=(ops.row, source), device_id_type=MESH,
        ).wait_recv()
    everything = jnp.concatenate([gathered[p] for p in range(ops.cols)], axis=1)
    solved = lax.dot_general(
        everything, inverse[...], (((1,), (1,)), ((), ())), preferred_element_type=F32
    )
    third.ref["uout"][...] = solved.astype(BF16)
    start(third.sends)
    while second_weights:
        start(second_weights.pop(0))

    def into_coarse_vector(level):
        def put(b, x):
            level.ref["uout"][:, b * bs : (b + 1) * bs] = x.astype(BF16)

        return put

    third.finish(into_coarse_vector(second))
    start(second.sends)
    second.finish(into_coarse_vector(fine))
    fine.up(out)
    for copy in ops.copies:
        copy.drain()
    for copy in sends:
        copy.wait_send()


def on_device(
    right_sides,
    weights_fine, columns_fine, degree_fine, owners_fine, slots_fine,
    weights_second, columns_second, degree_second, owners_second, slots_second,
    weights_third, columns_third, degree_third, owners_third, slots_third,
    coarse_inverse,
):
    n0, r, bs = right_sides.shape
    n1, n2 = weights_second.shape[0], weights_third.shape[0]
    k = weights_fine.shape[1]
    c3, m3 = coarse_inverse.shape
    cols = lax.axis_size("col")
    sizes = ((n0, n1 * bs), (n1, n2 * bs), (n2, c3))
    merged = lambda w: w.reshape(w.shape[0], k * bs, bs)
    args = [right_sides, coarse_inverse]
    for w, c, d, o, s in (
        (weights_fine, columns_fine, degree_fine, owners_fine, slots_fine),
        (weights_second, columns_second, degree_second, owners_second, slots_second),
        (weights_third, columns_third, degree_third, owners_third, slots_third),
    ):
        args += [c.T if c.shape[0] >= 4 else c, merged(w), d, o, s]
    specs = [pl.BlockSpec(memory_space=pltpu.HBM)] * len(args)
    vmem = pltpu.VMEM
    vector = lambda *lead: vmem((*lead, r, bs), BF16)

    def shared(n, t, window, ways, res, hot):
        return [
            vmem((n, k * bs, bs), BF16),
            vmem((n, bs), F32),
            vmem((n, bs), jnp.int32),
            vmem((n, bs), jnp.int32),
            vmem((n, 8, bs), F32),
            vmem((n, 8, bs), F32),
            vmem((window, r, bs), F32),
            *[vector(window)] * 4,
            vmem((res[0] * r, res[1] * bs), BF16),
            vmem((t, hot * bs), BF16),
            vmem((r, t), BF16),
            vmem((ways, r, t), BF16),
        ]

    def small(n, weights, degrees, source):
        m = min(n, 2)
        return [
            vmem((n, r, bs), F32),
            vmem((degrees, m, r, bs), source),
            vmem((weights, m, k * bs, bs), BF16),
            vmem((weights, n, bs), jnp.int32),
            vmem((weights, n, bs), jnp.int32),
            vmem((degrees, m, 8, bs), F32),
            vmem((degrees, m, 8, bs), F32),
        ]

    scratch = shared(n0, n1 * bs, n0, 2, (3, n0), n0)
    scratch += [vector(6)] * 8
    scratch += [vector(3, n1), vector(2, n1), vmem((n1, r, bs), F32), vector(2, 2), vector(2, 2)]
    scratch += shared(n1, n2 * bs, n1 + 8, 4, (3, n1), n1 + 8)
    scratch += small(n1, 2, 2, F32)
    scratch += [vector(2, n2), vector(2, n2), vmem((n2, r, bs), F32), vector(2, 4)]
    scratch += shared(n2, c3, n2 + 12, 6, (1, n2 + 4), n2 + 8)
    scratch += small(n2, 4, 6, BF16)
    scratch += [vector(n2)]
    scratch += [pltpu.SMEM((k, n0), jnp.int32)]
    scratch += [pltpu.SMEM((k, n1), jnp.int32)] * 3
    scratch += [pltpu.SMEM((n2, k), jnp.int32)] * 5
    scratch += [
        vector(n0),
        vmem((c3, m3), BF16),
        vmem((cols, r, c3), BF16),
        pltpu.SemaphoreType.DMA((140,)),
        pltpu.SemaphoreType.DMA((140,)),
        pltpu.SemaphoreType.DMA((cols,)),
        pltpu.SemaphoreType.DMA((cols,)),
        pltpu.SemaphoreType.DMA((24,)),
    ]
    return pl.pallas_call(
        functools.partial(kernel, sizes, r, bs, k),
        out_shape=jax.ShapeDtypeStruct((n0, r, bs), F32),
        in_specs=specs,
        out_specs=pl.BlockSpec(memory_space=pltpu.VMEM),
        scratch_shapes=scratch,
        compiler_params=pltpu.CompilerParams(
            collective_id=0, has_side_effects=True, vmem_limit_bytes=48 * 1024 * 1024
        ),
        name="vcycle",
    )(*[pltpu.with_memory_space_constraint(a, pltpu.HBM) for a in args])


def solution(mesh):
    whole = ("row", "col")
    vector, matrix, table = P(whole, None, None), P(whole, None, None, None), P(whole, None)
    level = (matrix, table, table, table, table)
    return jax.shard_map(
        on_device,
        mesh=mesh,
        in_specs=(vector, *level, *level, *level, table),
        out_specs=vector,
        check_vma=False,
    )
```

time: 98 us -> 80.7 us (0.82)
  the two profiles are of different devices: /device:TPU:3 before, /device:TPU:1 now
where the time goes in v2:
time: 80.7 us; the launch traced here: 80.5 us
  Pallas kernels  79.5 us (99%)
  local copies, waits for them, and re-layouts  0.97 us (1%)
    pallas_call x1, Pallas kernels, on_device(): pl.pallas_call(functools.partial(kernel, sizes, r, bs, k), out_shape=jax....  79.5 us

profile of v2, /device:TPU:1, one launch (start us, length us, event | category | flops | bytes accessed | tf_op | source)
XLA Modules:
  0.0 80.5 jit_solution(5276202720142196875)
XLA Ops:
  0.0 79.5 %vcycle.1 = f32[32,64,128]{2,1,0:T(8,128)S(1)} custom-call(bf16[32,64,128]{2,1,0:T(8,128)(2,1)} %refs_0_.1, bf16[128,1024]{1,0:T(8,128)(2,1)} %refs_1_.1, s32[3,32]{1,0:T(4,128)} %bitcast.8, bf16[32,384,128]{2,1,0:T(8,128)(2,1)} %bitcast.5, f32[32,128]{1,0:T(8,128)} %refs_4_.1, s32[32,128]{1,0:T(8,128)} %refs_5_.1, s32[32,128]{1,0:T(8,128)} %refs_6_.1, ...), custom_call_target="tpu_custom_call" | custom-call | tf_op jit(solution)/shard_map/vcycle/pallas_call | solution.py:863
  79.5 1.0 %copy.19 = f32[32,64,128]{2,1,0:T(8,128)} copy(f32[32,64,128]{2,1,0:T(8,128)S(1)} %vcycle.1) | data formatting | bytes 2097152

commit v3 on v2

--- a/solution.py
+++ b/solution.py
@@ -9,8 +9,11 @@
 
 F32 = jnp.float32
 BF16 = jnp.bfloat16
+F8 = jnp.float8_e4m3fn
 MESH = pl.DeviceIdType.MESH
 DAMPING = 0.8
+THIRD_SLOTS = (2, 1, 2, 1)
+SECOND_SLOTS = (1, 1, 2, 2)
 
 
 def loop(low, high, body, unroll=4):
@@ -68,6 +71,15 @@
 
     def drain(self):
         pl.when(self.ops.has(self.delta))(lambda: self.descriptor.wait_send())
+
+
+class Slots:
+    def __init__(self, groups, counts):
+        self.groups, self.counts = list(groups), list(counts)
+
+    def send(self):
+        for _ in range(self.counts.pop(0)):
+            start(self.groups.pop(0))
 
 
 def start(copies):
@@ -130,10 +142,14 @@
     def spread(self, row):
         return jnp.broadcast_to(row, (self.r, self.bs))
 
-    def hot(self, row):
-        slots = jnp.broadcast_to(row, (self.t, self.bs))
-        index = lax.broadcasted_iota(jnp.int32, (self.t, self.bs), 0)
-        return jnp.where(index == slots, 1.0, 0.0).astype(BF16)
+    def put_hot(self, row, columns):
+        size = 32
+        index = lax.broadcasted_iota(jnp.int32, (size, self.bs), 0)
+        away = (index - jnp.broadcast_to(row, (size, self.bs))).astype(jnp.int16)
+        one, zero = jnp.ones((size, self.bs), BF16), jnp.zeros((size, self.bs), BF16)
+        for low in range(0, self.t, size):
+            hit = jnp.where(away == jnp.int16(-low), one, zero)
+            self.ref["oh"][low : low + size, columns] = hit.astype(F8)
 
     def put_residual(self, columns, res, rel):
         rows = self.r
@@ -209,11 +225,13 @@
         left = jnp.concatenate(picked, axis=1)
         return jnp.dot(left, self.ref["w"][b], preferred_element_type=F32) * self.scale
 
-    def apply(self, i, body):
+    def apply(self, i, body, meanwhile=None):
         grouped(*self.inner(), lambda b: self.product(i, b, "inner"), body)
         n = self.n
         self.ref[f"lo{i}"][2:6] = self.ref[f"vb{i}"][0:4]
         self.ref[f"hi{i}"][0:4] = self.ref[f"vb{i}"][n - 4 : n]
+        if meanwhile is not None:
+            meanwhile()
         wait(self.halo[i])
         made = [self.product(i, b, "low" if b < 2 else "high") for b in self.edges()]
         for b, product in zip(self.edges(), made):
@@ -240,13 +258,25 @@
         self.put_residual(self.at(b), res, self.owner(b))
 
     def make_onehot(self, b):
-        self.ref["oh"][:, self.at(b)] = self.hot(self.ref["slot"][pl.ds(b, 1), :])
+        self.put_hot(self.ref["slot"][pl.ds(b, 1), :], self.at(b))
+
+    def restrict_inner(self):
+        bs = self.bs
+        inner = slice(2 * bs, (self.n - 2) * bs)
+        for j in self.tiles:
+            at = slice(2 * j * bs, (2 * j + 2) * bs)
+            self.ref["part"][:, at] = self.restricted(
+                self.ref["res"][:, inner], self.ref["oh"][at, inner]
+            )
 
     def restrict(self):
         r, bs = self.r, self.bs
+        ends = (slice(0, 2 * bs), slice((self.n - 2) * bs, self.n * bs))
         for j in self.tiles:
             at = slice(2 * j * bs, (2 * j + 2) * bs)
-            value = self.restricted(self.ref["res"][...], self.ref["oh"][at, :])
+            value = self.ref["part"][:, at]
+            for end in ends:
+                value += self.restricted(self.ref["res"][:, end], self.ref["oh"][at, end])
             for half in range(2):
                 b = 2 * j + half
                 part = value[:, half * bs : (half + 1) * bs]
@@ -361,8 +391,11 @@
                     group.append(ops.copy(ref["w"].at[source, part], ref["wn"].at[at, j, part], -d))
                 self.weights.append(group)
         self.sends = [
-            ops.copy(ref["uout"], ref["uin"].at[at], -d) for at, d in enumerate(send_ways)
+            ops.copy(ref["uout"], ref["uin"].at[at], -d) for at, d in self.far_first(send_ways)
         ]
+
+    def far_first(self, ways):
+        return sorted(enumerate(ways), key=lambda pair: -abs(pair[1]))
 
     def edge(self, d):
         return slice(self.n - self.m, self.n) if d < 0 else slice(0, self.m)
@@ -410,7 +443,7 @@
     def make_onehots(self, reach):
         for b in range(-reach, self.n + reach):
             at = (b + reach) * self.bs
-            self.ref["oh"][:, at : at + self.bs] = self.hot(self.table("slot", b))
+            self.put_hot(self.table("slot", b), slice(at, at + self.bs))
 
     def product(self, i, b):
         buf = self.ref[f"vb{i}"]
@@ -474,10 +507,6 @@
                 out(b, x)
 
         return body
-
-    def up(self, out):
-        start(self.sends)
-        return self.sends
 
     def clear_ends(self):
         for at, d in enumerate(self.weight_ways):
@@ -588,7 +617,8 @@
         super().__init__(*args, 6, (-2, -1, 1, 2), (-3, -2, -1, 1, 2, 3), (-3, -2, -1, 1, 2, 3))
         ref, ops = self.ref, self.ops
         self.sources = [
-            ops.copy(ref["fout"], ref["fn"].at[at], -d) for at, d in enumerate(self.degree_ways)
+            ops.copy(ref["fout"], ref["fn"].at[at], -d)
+            for at, d in self.far_first(self.degree_ways)
         ]
 
     def down(self, into):
@@ -620,7 +650,7 @@
 LEVEL_HBM = ("w", "deg", "own", "slot")
 SHARED = ("w", "deg", "own", "slot", "g", "gi", "x", "vb0", "vb1", "vb2", "vb3", "res", "oh", "uout", "uin")
 FINE = SHARED + (
-    "lo0", "lo1", "lo2", "lo3", "hi0", "hi1", "hi2", "hi3", "rout", "rin", "rown", "near", "far",
+    "lo0", "lo1", "lo2", "lo3", "hi0", "hi1", "hi2", "hi3", "rout", "rin", "rown", "near", "far", "part",
 )
 SMALL = SHARED + ("f", "fn", "wn", "ownn", "slotn", "gn", "gin")
 SECOND = SMALL + ("rout", "rin", "rown", "vin")
@@ -665,10 +695,12 @@
     early.append(load(rhs_hbm, rhs))
     for level in range(3):
         early.append(load(columns_hbm[level], columns[level][0]))
+    heavy = load(hbm[2]["w"], scratch[2]["w"])
     middle = load(hbm[0]["w"].at[2 : n - 2], scratch[0]["w"].at[2 : n - 2])
     later = [load(hbm[0][name], scratch[0][name]) for name in ("own", "slot")]
     for position in (1, 2):
-        later += [load(hbm[position][name], scratch[position][name]) for name in LEVEL_HBM]
+        names = LEVEL_HBM[position - 1 :]
+        later += [load(hbm[position][name], scratch[position][name]) for name in names]
     last = load(inverse_hbm, inverse)
 
     barrier = pltpu.get_barrier_semaphore()
@@ -696,27 +728,25 @@
     made = [fine.weight_sums(b) for b in fine.edges()]
     for b, total in zip(fine.edges(), made):
         diagonal_and_start(b, total)
+    pl.semaphore_wait(barrier, expected)
+    start(fine.halo[0])
+    third_weights = Slots(third.weights, THIRD_SLOTS)
+    second_weights = Slots(second.weights, SECOND_SLOTS)
+    heavy.wait()
+    third_weights.send()
     middle.wait()
     grouped(*fine.inner(), fine.weight_sums, diagonal_and_start)
     for copy in later:
         copy.wait()
     for level in (second, third):
         grouped(0, level.n, level.weight_sums, level.put_diagonal, 8)
-    pl.semaphore_wait(barrier, expected)
-
-    start(fine.halo[0])
     start(second.tables)
     start(third.tables)
-    third_weights = list(third.weights)
-    for _ in range(2):
-        start(third_weights.pop(0))
-    loop(0, n // 2, fine.make_onehot, 1)
+    loop(0, n, fine.make_onehot, 2)
     fine.apply(0, fine.first_sweep)
     start(fine.halo[1])
-    for _ in range(2):
-        start(third_weights.pop(0))
-    loop(n // 2, n, fine.make_onehot, 1)
-    fine.apply(1, fine.residual)
+    third_weights.send()
+    fine.apply(1, fine.residual, fine.restrict_inner)
     fine.restrict()
     for level in (second, third):
         wait(level.tables)
@@ -724,18 +754,12 @@
         level.make_onehots(4)
     fine.received(second)
 
-    def rest_of_weights():
-        while third_weights:
-            start(third_weights.pop(0))
-
-    second.down(third, rest_of_weights)
-    second_weights = list(second.weights)
-    for _ in range(2):
-        start(second_weights.pop(0))
+    second.down(third, third_weights.send)
+    third_weights.send()
+    second_weights.send()
     second.received(third)
     start(third.sources)
-    for _ in range(2):
-        start(second_weights.pop(0))
+    second_weights.send()
 
     def into_coarse(value):
         gathered[ops.col] = value.astype(BF16)
@@ -752,6 +776,7 @@
         )
         copy.start()
         sends.append(copy)
+    second_weights.send()
     last.wait()
     for step in range(1, ops.cols):
         source = lax.rem(ops.col + ops.cols - step, ops.cols)
@@ -766,8 +791,7 @@
     )
     third.ref["uout"][...] = solved.astype(BF16)
     start(third.sends)
-    while second_weights:
-        start(second_weights.pop(0))
+    second_weights.send()
 
     def into_coarse_vector(level):
         def put(b, x):
@@ -821,7 +845,7 @@
             vmem((window, r, bs), F32),
             *[vector(window)] * 4,
             vmem((res[0] * r, res[1] * bs), BF16),
-            vmem((t, hot * bs), BF16),
+            vmem((t, hot * bs), F8),
             vmem((r, t), BF16),
             vmem((ways, r, t), BF16),
         ]
@@ -841,6 +865,7 @@
     scratch = shared(n0, n1 * bs, n0, 2, (3, n0), n0)
     scratch += [vector(6)] * 8
     scratch += [vector(3, n1), vector(2, n1), vmem((n1, r, bs), F32), vector(2, 2), vector(2, 2)]
+    scratch += [vmem((3 * r, n1 * bs), F32)]
     scratch += shared(n1, n2 * bs, n1 + 8, 4, (3, n1), n1 + 8)
     scratch += small(n1, 2, 2, F32)
     scratch += [vector(2, n2), vector(2, n2), vmem((n2, r, bs), F32), vector(2, 4)]

time: 80.7 us -> 76.7 us (0.950)
  the two profiles are of different devices: /device:TPU:1 before, /device:TPU:3 now
where the time goes in v3:
time: 76.7 us; the launch traced here: 76.6 us
  Pallas kernels  75.6 us (99%)
  local copies, waits for them, and re-layouts  0.97 us (1%)
    pallas_call x1, Pallas kernels, on_device(): pl.pallas_call(functools.partial(kernel, sizes, r, bs, k), out_shape=jax....  75.6 us

profile of v3, /device:TPU:3, one launch (start us, length us, event | category | flops | bytes accessed | tf_op | source)
XLA Modules:
  0.0 76.6 jit_solution(18050349934656155578)
XLA Ops:
  0.0 75.6 %vcycle.1 = f32[32,64,128]{2,1,0:T(8,128)S(1)} custom-call(bf16[32,64,128]{2,1,0:T(8,128)(2,1)} %refs_0_.1, bf16[128,1024]{1,0:T(8,128)(2,1)} %refs_1_.1, s32[3,32]{1,0:T(4,128)} %bitcast.8, bf16[32,384,128]{2,1,0:T(8,128)(2,1)} %bitcast.5, f32[32,128]{1,0:T(8,128)} %refs_4_.1, s32[32,128]{1,0:T(8,128)} %refs_5_.1, s32[32,128]{1,0:T(8,128)} %refs_6_.1, ...), custom_call_target="tpu_custom_call" | custom-call | tf_op jit(solution)/shard_map/vcycle/pallas_call | solution.py:888
  75.6 1.0 %copy.19 = f32[32,64,128]{2,1,0:T(8,128)} copy(f32[32,64,128]{2,1,0:T(8,128)S(1)} %vcycle.1) | data formatting | bytes 2097152

commit v4 on v3

--- a/solution.py
+++ b/solution.py
@@ -741,11 +741,11 @@
     for level in (second, third):
         grouped(0, level.n, level.weight_sums, level.put_diagonal, 8)
     start(second.tables)
-    start(third.tables)
     loop(0, n, fine.make_onehot, 2)
     fine.apply(0, fine.first_sweep)
     start(fine.halo[1])
     third_weights.send()
+    start(third.tables)
     fine.apply(1, fine.residual, fine.restrict_inner)
     fine.restrict()
     for level in (second, third):

time: 76.7 us -> 76.1 us (level)
  no operation moved by 1% of the time
where the time goes in v4:
time: 76.1 us; the launch traced here: 75.9 us
  Pallas kernels  75 us (99%)
  local copies, waits for them, and re-layouts  0.97 us (1%)
    pallas_call x1, Pallas kernels, on_device(): pl.pallas_call(functools.partial(kernel, sizes, r, bs, k), out_shape=jax....  75 us

profile of v4, /device:TPU:3, one launch (start us, length us, event | category | flops | bytes accessed | tf_op | source)
XLA Modules:
  0.0 75.9 jit_solution(8465524133958299471)
XLA Ops:
  0.0 75.0 %vcycle.1 = f32[32,64,128]{2,1,0:T(8,128)S(1)} custom-call(bf16[32,64,128]{2,1,0:T(8,128)(2,1)} %refs_0_.1, bf16[128,1024]{1,0:T(8,128)(2,1)} %refs_1_.1, s32[3,32]{1,0:T(4,128)} %bitcast.8, bf16[32,384,128]{2,1,0:T(8,128)(2,1)} %bitcast.5, f32[32,128]{1,0:T(8,128)} %refs_4_.1, s32[32,128]{1,0:T(8,128)} %refs_5_.1, s32[32,128]{1,0:T(8,128)} %refs_6_.1, ...), custom_call_target="tpu_custom_call" | custom-call | tf_op jit(solution)/shard_map/vcycle/pallas_call | solution.py:888
  75.0 1.0 %copy.19 = f32[32,64,128]{2,1,0:T(8,128)} copy(f32[32,64,128]{2,1,0:T(8,128)S(1)} %vcycle.1) | data formatting | bytes 2097152
